TPU v7x, 32 devices: a whole 2x2x4 slice. The times are simulated.
32 devices in a mesh: lat: 4 (over y, x), lon: 8 (over z, core).
Axes of the slice: x: 2, y: 2, z: 4, core: 2. Of those that a mesh axis runs over, the one named last changes fastest.
Arguments:
- adjoint_in: bfloat16 [8, 100, 8, 1024], P(None, None, 'lat', 'lon'), may hold values from -6 to 6
- state: bfloat16 [2, 8, 100, 8, 1024], P(None, None, None, 'lat', 'lon'), may hold values from 0.29882812 to 1
- inverses: bfloat16 [3, 8, 100, 100], replicated
- courant_lon: float32 [8, 1024], P('lat', 'lon'), may hold values from 0.1 to 0.4
- courant_lat: float32 [8, 1024], P('lat', 'lon'), may hold values from 0.1 to 0.4
- emission: float32 [100, 8, 1024], P(None, 'lat', 'lon'), may hold values from 0.02 to 0.2
- region_id: int32 [8, 1024], P('lat', 'lon'), may hold values from 0 to 31, as said below
- stiffness: int32 [8, 8, 1024], P(None, 'lat', 'lon'), may hold values from 1 to 3
Outputs:
- adjoint_out: bfloat16 [8, 100, 8, 1024], P(None, None, 'lat', 'lon')
- emission_grad: float32 [32, 100], P(('lat', 'lon'))
Inputs may be any that keep to these rules, and one draw needn't show every extreme that they name: `region_id`: constant on aligned tiles of 2 x 2 columns.
All inputs are finite; a program needn't handle non-finite values.
Results may differ from a plain program's by a relative error of at most 0.0048.
Values sent between devices are 32-bit elements; how exact they have to be, the bound alone decides.
A program may use at most 64 MiB of HBM per device.

v0:
```python
import jax
import jax.numpy as jnp
from jax import lax
from jax.sharding import PartitionSpec as P

STEPS = 3
NWIN = 2
ADV = 2
REG_DEV = 1


def shifted(block, axis, distance):
    devices = range(lax.axis_size(axis))
    route = [((i - distance) % len(devices), i) for i in devices]
    return lax.ppermute(block, axis, route)


def from_behind(block, axis, distance):
    devices = range(lax.axis_size(axis))
    route = [(i - distance, i) for i in devices if i - distance in devices]
    return lax.ppermute(block, axis, route)


def advect(lam, clon, clat, east, south):
    right = jnp.concatenate([lam[:, :, :, 1:], east], axis=3)
    down = jnp.concatenate([lam[:, :, 1:, :], south], axis=2)
    return (1.0 - clon - clat) * lam + clat * down + clon * right


def transport_each(lam, courant_lon, courant_lat):
    for k in range(ADV):
        east = shifted(lam[:, :, :, :1], "lon", -1)
        south = from_behind(lam[:, :, :1, :], "lat", -1)
        lam = advect(lam, courant_lon, courant_lat, east, south)
    return lam


def transposed(mats, right_side):
    return lax.dot_general(
        mats, right_side, (((1,), (1,)), ((0,), (0,))), preferred_element_type=jnp.float32
    )


def chemistry(lam, factor, inverses, stiffness):
    levels, spec, rows, cols = lam.shape
    flat = lam.reshape(levels, spec, rows * cols)
    yfac = factor.reshape(levels, spec, rows * cols)
    live = stiffness.reshape(levels, 1, rows * cols)
    for s in reversed(range(STEPS)):
        mats = inverses[s]

        def advance(values, mats=mats, s=s):
            first = transposed(mats, values.astype(jnp.bfloat16))
            second = transposed(mats, (first * yfac).astype(jnp.bfloat16))
            third = transposed(mats, (second * yfac).astype(jnp.bfloat16))
            cand = 0.4 * values + 0.3 * first + 0.2 * second + 0.1 * third
            return jnp.where(live > s, cand, values)

        flat = lax.cond(jnp.any(stiffness > s), advance, lambda values: values, flat)
    return flat.reshape(levels, spec, rows, cols)


def per_device(
    adjoint_in, state, inverses, courant_lon, courant_lat, emission, region_id, stiffness
):
    lam = adjoint_in.astype(jnp.float32)
    surface = jnp.zeros(emission.shape, jnp.float32)
    for window in reversed(range(NWIN)):
        lam = transport_each(lam, courant_lon, courant_lat)
        lam = chemistry(lam, state[window], inverses, stiffness)
        surface = surface + lam[0]
    spec = emission.shape[0]
    regions = REG_DEV * lax.axis_size("lat") * lax.axis_size("lon")
    contrib = (surface * emission).reshape(spec, -1)
    labels = lax.broadcasted_iota(jnp.int32, (regions, contrib.shape[1]), 0)
    onehot = (region_id.reshape(1, -1) == labels).astype(jnp.float32)
    partial_value = lax.dot_general(
        onehot,
        contrib,
        (((1,), (1,)), ((), ())),
        precision=lax.Precision.HIGHEST,
        preferred_element_type=jnp.float32,
    )
    total = lax.psum(partial_value, ("lat", "lon"))
    share = REG_DEV
    grad = lax.dynamic_slice_in_dim(total, lax.axis_index(("lat", "lon")) * share, share, 0)
    return (lam.astype(jnp.bfloat16), grad)


def solution(mesh):
    in_specs = (
        P(None, None, "lat", "lon"),
        P(None, None, None, "lat", "lon"),
        P(),
        P("lat", "lon"),
        P("lat", "lon"),
        P(None, "lat", "lon"),
        P("lat", "lon"),
        P(None, "lat", "lon"),
    )
    out_specs = (P(None, None, "lat", "lon"), P(("lat", "lon"), None))
    return jax.shard_map(
        per_device, mesh=mesh, in_specs=in_specs, out_specs=out_specs, check_vma=False
    )
```

profile of v0, /device:TPU:0, one launch (start us, length us, event | category | flops | bytes accessed | tf_op | source)
XLA Modules:
  0.0 117.9 jit_solution(164117389838447661)
XLA Ops:
  2.5 1.3 %collective-permute-start = (f32[8,100,1,128]{3,0,2,1:T(8,128)}, f32[8,100,1,128]{3,0,2,1:T(8,128)}, u32[]{:S(2)}, u32[]{:S(2)}) collective-permute-start(f32[8,100,1,128]{3,0,2,1:T(8,128)} %get-tuple-element.166), channel_id=1, source_target_pairs={{8,0},{16,8},{24,16},{9,1},{17,9},{25,17},{10,2},{18,10},{26,18},{... | collective-permute-start | bytes 1228808 | tf_op jit(solution)/shard_map/ppermute | solution.py:21
  4.2 4.5 %collective-permute-start.1 = (f32[8,100,2,1]{1,0,3,2:T(8,128)S(1)}, f32[8,100,2,1]{1,0,3,2:T(8,128)S(1)}, u32[]{:S(2)}, u32[]{:S(2)}) collective-permute-start(f32[8,100,2,1]{1,0,3,2:T(8,128)S(1)} %copy.34), channel_id=1, source_target_pairs={{1,0},{2,1},{3,2},{4,3},{5,4},{6,5},{7,6},{0,7},{9,8},{10,9},{11,1... | collective-permute-start | bytes 19208 | tf_op jit(solution)/shard_map/ppermute | solution.py:15
  10.5 6.6 %collective-permute-done = f32[8,100,1,128]{3,0,2,1:T(8,128)} collective-permute-done((f32[8,100,1,128]{3,0,2,1:T(8,128)}, f32[8,100,1,128]{3,0,2,1:T(8,128)}, u32[]{:S(2)}, u32[]{:S(2)}) %collective-permute-start) | collective-permute-done | bytes 409632 | tf_op jit(solution)/shard_map/ppermute | solution.py:21
  17.1 1.3 %fusion.65 = f32[8,100,2,128]{3,0,2,1:T(8,128)S(1)} fusion(f32[8,100,1,128]{3,0,2,1:T(8,128)} %collective-permute-done, f32[8,100,1,128]{3,0,2,1:T(8,128)S(1)} %get-tuple-element.165, f32[8,100,2,1]{3,0,2,1:T(8,128)S(1)} %copy.35, f32[8,100,2,127]{3,0,2,1:T(8,128)S(1)} %slice.99, f32[2,128]{1,0:T(2,128)S(1)} %copy-done.7, f32[2,128]{1,0:T(2,128)S(1)} %copy-done.8, ...), kind=kLoop, calls=%fused_computation.86 | loop fusion | flops 1638400 | bytes 2870272 | tf_op jit(solution)/shard_map/add | solution.py:27
  19.4 1.4 %collective-permute-start.2 = (f32[8,100,1,128]{3,0,2,1:T(8,128)}, f32[8,100,1,128]{3,0,2,1:T(8,128)}, u32[]{:S(2)}, u32[]{:S(2)}) collective-permute-start(f32[8,100,1,128]{3,0,2,1:T(8,128)} %get-tuple-element.164), channel_id=1, source_target_pairs={{8,0},{16,8},{24,16},{9,1},{17,9},{25,17},{10,2},{18,10},{26,18},{... | collective-permute-start | bytes 1228808 | tf_op jit(solution)/shard_map/ppermute | solution.py:21
  20.9 1.3 %fusion.79 = (bf16[1,8,100,2,128]{4,3,2,1,0:T(2,128)(2,1)}, bf16[1,8,100,2,128]{4,3,2,1,0:T(2,128)(2,1)S(1)}) fusion(bf16[2,8,100,2,128]{4,3,2,1,0:T(2,128)(2,1)S(1)} %copy-done.3), kind=kLoop, calls=%fused_computation.122 | loop fusion | bytes 1638400 | tf_op jit(solution)/shard_map/slice | solution.py:70
  22.6 2.4 %collective-permute-start.3 = (f32[8,100,2,1]{1,0,3,2:T(8,128)S(1)}, f32[8,100,2,1]{1,0,3,2:T(8,128)}, u32[]{:S(2)}, u32[]{:S(2)}) collective-permute-start(f32[8,100,2,1]{1,0,3,2:T(8,128)S(1)} %copy.36), channel_id=1, source_target_pairs={{1,0},{2,1},{3,2},{4,3},{5,4},{6,5},{7,6},{0,7},{9,8},{10,9},{11,1... | collective-permute-start | bytes 19208 | tf_op jit(solution)/shard_map/ppermute | solution.py:15
  30.0 3.0 %collective-permute-done.2 = f32[8,100,1,128]{3,0,2,1:T(8,128)} collective-permute-done((f32[8,100,1,128]{3,0,2,1:T(8,128)}, f32[8,100,1,128]{3,0,2,1:T(8,128)}, u32[]{:S(2)}, u32[]{:S(2)}) %collective-permute-start.2) | collective-permute-done | bytes 409632 | tf_op jit(solution)/shard_map/ppermute | solution.py:21
  33.0 1.4 %fusion.68 = f32[8,100,256]{2,0,1:T(8,128)S(1)} fusion(f32[8,100,1,128]{3,0,2,1:T(8,128)} %collective-permute-done.2, f32[8,100,1,128]{3,0,2,1:T(8,128)} %get-tuple-element.163, f32[8,100,2,1]{3,0,2,1:T(8,128)S(1)} %copy.37, f32[8,100,2,127]{3,0,2,1:T(8,128)S(1)} %slice.103, f32[8,100,2,128]{3,0,2,1:T(8,128)S(1)} %fusion.65, f32[2,128]{1,0:T(2,128)S(1)} %copy-done.7, ...), kind=kLoop, calls=%fused_computation.91 | loop fusion | flops 1433600 | bytes 3279872 | tf_op jit(solution)/shard_map/reshape | solution.py:46
  34.4 1.3 %conditional.6 = (f32[8,100,256]{2,1,0:T(8,128)S(1)}) conditional(s32[]{:T(128)} %convert_element_type.102, (f32[8,100,256]{2,0,1:T(8,128)S(1)}) %tuple.65, (s32[8,1,256]{2,0,1:T(8,128)S(1)}, f32[8,100,256]{2,0,1:T(8,128)S(1)}, bf16[8,100,100]{1,2,0:T(8,128)(2,1)S(1)}, bf16[8,100,256]{2,0,1:T(8,128)(2,1)S(1)}) %tuple.94), branch_computations={%region_3.4_spmd, %region_4.5_spmd} | conditional | flops 125749248 | bytes 7865096 | solution.py:59
  35.8 1.3 %conditional.7 = (f32[8,100,256]{2,1,0:T(8,128)S(1)}) conditional(s32[]{:T(128)} %convert_element_type.101, f32[8,100,256]{2,1,0:T(8,128)S(1)} %get-tuple-element.170, (s32[8,1,256]{2,0,1:T(8,128)S(1)}, f32[8,100,256]{2,1,0:T(8,128)S(1)}, bf16[8,100,100]{1,2,0:T(8,128)(2,1)S(1)}, bf16[8,100,256]{2,0,1:T(8,128)(2,1)S(1)}) %tuple.98), branch_computations={%region_5.6_spmd, %region_6.7_spmd} | conditional | flops 125954048 | bytes 7865096 | solution.py:59
  37.1 1.3 %conditional.8 = (f32[8,100,256]{2,1,0:T(8,128)S(1)}) conditional(s32[]{:T(128)} %convert_element_type.100, f32[8,100,256]{2,1,0:T(8,128)S(1)} %get-tuple-element.171, (s32[8,1,256]{2,0,1:T(8,128)S(1)}, f32[8,100,256]{2,1,0:T(8,128)S(1)}, bf16[8,100,100]{1,2,0:T(8,128)(2,1)S(1)}, bf16[8,100,256]{2,0,1:T(8,128)(2,1)S(1)}) %tuple.96), branch_computations={%region_7.8_spmd, %region_8.9_spmd} | conditional | flops 125954048 | bytes 7865096 | solution.py:59
  39.5 1.3 %collective-permute-start.4 = (f32[8,100,1,128]{3,0,2,1:T(8,128)}, f32[8,100,1,128]{3,0,2,1:T(8,128)}, u32[]{:S(2)}, u32[]{:S(2)}) collective-permute-start(f32[8,100,1,128]{3,0,2,1:T(8,128)} %get-tuple-element.162), channel_id=1, source_target_pairs={{8,0},{16,8},{24,16},{9,1},{17,9},{25,17},{10,2},{18,10},{26,18},{... | collective-permute-start | bytes 1228808 | tf_op jit(solution)/shard_map/ppermute | solution.py:21
  42.6 1.3 %collective-permute-done.5 = f32[8,100,2,1]{1,0,3,2:T(8,128)} collective-permute-done((f32[8,100,2,1]{1,0,3,2:T(8,128)}, f32[8,100,2,1]{1,0,3,2:T(8,128)}, u32[]{:S(2)}, u32[]{:S(2)}) %collective-permute-start.5) | collective-permute-done | bytes 6432 | tf_op jit(solution)/shard_map/ppermute | solution.py:15
  43.9 2.0 %copy.50 = f32[8,100,2,1]{3,0,2,1:T(8,128)} copy(f32[8,100,2,1]{1,0,3,2:T(8,128)} %collective-permute-done.5) | data formatting | bytes 12800 | tf_op jit(solution)/shard_map/ppermute | solution.py:15
  45.9 6.2 %collective-permute-done.4 = f32[8,100,1,128]{3,0,2,1:T(8,128)} collective-permute-done((f32[8,100,1,128]{3,0,2,1:T(8,128)}, f32[8,100,1,128]{3,0,2,1:T(8,128)}, u32[]{:S(2)}, u32[]{:S(2)}) %collective-permute-start.4) | collective-permute-done | bytes 409632 | tf_op jit(solution)/shard_map/ppermute | solution.py:21
  52.1 1.7 %multiply_add_fusion = f32[8,100,2,128]{3,0,2,1:T(8,128)S(1)} fusion(f32[8,100,1,128]{3,0,2,1:T(8,128)} %collective-permute-done.4, f32[8,100,1,128]{3,0,2,1:T(8,128)S(1)} %get-tuple-element.161, f32[2,128]{1,0:T(2,128)S(1)} %copy-done.7, f32[2,128]{1,0:T(2,128)S(1)} %copy-done.8, f32[2,128]{1,0:T(2,128)S(1)} %copy-done.11, f32[8,100,2,1]{3,0,2,1:T(8,128)} %copy.50, ...), kind=kLoop, calls=%fused_computation.107 | loop fusion | flops 1433600 | bytes 3279872 | tf_op jit(solution)/shard_map/add | solution.py:27
  60.1 2.0 %copy.52 = f32[8,100,2,1]{3,0,2,1:T(8,128)} copy(f32[8,100,2,1]{1,0,3,2:T(8,128)} %collective-permute-done.7) | data formatting | bytes 12800 | tf_op jit(solution)/shard_map/ppermute | solution.py:15
  62.1 4.4 %collective-permute-done.6 = f32[8,100,1,128]{3,0,2,1:T(8,128)} collective-permute-done((f32[8,100,1,128]{3,0,2,1:T(8,128)}, f32[8,100,1,128]{3,0,2,1:T(8,128)}, u32[]{:S(2)}, u32[]{:S(2)}) %collective-permute-start.6) | collective-permute-done | bytes 409632 | tf_op jit(solution)/shard_map/ppermute | solution.py:21
  67.2 2.5 %fusion.71 = f32[8,100,256]{2,0,1:T(8,128)S(1)} fusion(f32[8,100,1,128]{3,0,2,1:T(8,128)} %collective-permute-done.6, f32[8,100,1,128]{3,0,2,1:T(8,128)} %get-tuple-element.159, f32[8,100,2,1]{3,0,2,1:T(8,128)} %copy.52, f32[8,100,2,127]{3,0,2,1:T(8,128)} %slice.111, f32[8,100,256]{2,1,0:T(8,128)S(1)} %get-tuple-element.172, ...), kind=kLoop, calls=%fused_computation.98 | loop fusion | flops 2867200 | bytes 4918272 | tf_op jit(solution)/shard_map/add | solution.py:27
  69.7 1.5 %conditional.9 = (f32[8,100,256]{2,1,0:T(8,128)S(1)}) conditional(s32[]{:T(128)} %convert_element_type.102, (f32[8,100,256]{2,0,1:T(8,128)S(1)}) %tuple.66, (s32[8,1,256]{2,0,1:T(8,128)S(1)}, f32[8,100,256]{2,0,1:T(8,128)S(1)}, bf16[8,100,100]{1,2,0:T(8,128)(2,1)S(1)}, bf16[8,100,256]{2,0,1:T(8,128)(2,1)S(1)}) %tuple.95), branch_computations={%region_9.10_spmd, %region_10.11_spmd} | conditional | flops 125749248 | bytes 7865096 | solution.py:59
  71.2 1.3 %conditional.10 = (f32[8,100,256]{2,1,0:T(8,128)S(1)}) conditional(s32[]{:T(128)} %convert_element_type.101, f32[8,100,256]{2,1,0:T(8,128)S(1)} %get-tuple-element.173, (s32[8,1,256]{2,0,1:T(8,128)S(1)}, f32[8,100,256]{2,1,0:T(8,128)S(1)}, bf16[8,100,100]{1,2,0:T(8,128)(2,1)S(1)}, bf16[8,100,256]{2,0,1:T(8,128)(2,1)S(1)}) %tuple.99), branch_computations={%region_11.12_spmd, %region_12.13_spmd} | conditional | flops 125954048 | bytes 7865096 | solution.py:59
  72.5 1.3 %conditional.11 = (f32[8,100,256]{2,1,0:T(8,128)S(1)}) conditional(s32[]{:T(128)} %convert_element_type.100, f32[8,100,256]{2,1,0:T(8,128)S(1)} %get-tuple-element.174, (s32[8,1,256]{2,0,1:T(8,128)S(1)}, f32[8,100,256]{2,1,0:T(8,128)S(1)}, bf16[8,100,100]{1,2,0:T(8,128)(2,1)S(1)}, bf16[8,100,256]{2,0,1:T(8,128)(2,1)S(1)}) %tuple.97), branch_computations={%region_13.14_spmd, %region_14.15_spmd} | conditional | flops 125954048 | bytes 7865096 | solution.py:59
  76.0 40.3 %psum.7 = f32[32,100]{1,0:T(8,128)S(1)} all-reduce(f32[32,100]{1,0:T(8,128)S(1)} %fusion.77), channel_id=1, replica_groups=mesh['lat'=4,'lon'=8] {'lat','lon'}, use_global_device_ids=true, to_apply=%region_15.16 | all-reduce | flops 3200 | bytes 25600 | tf_op jit(solution)/shard_map/psum | solution.py:84
  (92 shorter events, 29.6 us)
Async XLA Ops:
  2.5 14.6 %collective-permute-start = (f32[8,100,1,128]{3,0,2,1:T(8,128)}, f32[8,100,1,128]{3,0,2,1:T(8,128)}, u32[]{:S(2)}, u32[]{:S(2)}) collective-permute-start(f32[8,100,1,128]{3,0,2,1:T(8,128)} %get-tuple-element.166), channel_id=1, source_target_pairs={{8,0},{16,8},{24,16},{9,1},{17,9},{25,17},{10,2},{18,10},{26,18},{... | collective-permute-start | bytes 1228808 | tf_op jit(solution)/shard_map/ppermute | solution.py:21
  3.8 4.9 %copy-start.7 = (f32[2,128]{1,0:T(2,128)S(1)}, f32[2,128]{1,0:T(2,128)}, u32[]{:S(2)}) copy-start(f32[2,128]{1,0:T(2,128)} %param.23) | copy-start | bytes 3076
  3.8 4.9 %copy-start.8 = (f32[2,128]{1,0:T(2,128)S(1)}, f32[2,128]{1,0:T(2,128)}, u32[]{:S(2)}) copy-start(f32[2,128]{1,0:T(2,128)} %param.24) | copy-start | bytes 3076
  4.2 5.9 %collective-permute-start.1 = (f32[8,100,2,1]{1,0,3,2:T(8,128)S(1)}, f32[8,100,2,1]{1,0,3,2:T(8,128)S(1)}, u32[]{:S(2)}, u32[]{:S(2)}) collective-permute-start(f32[8,100,2,1]{1,0,3,2:T(8,128)S(1)} %copy.34), channel_id=1, source_target_pairs={{1,0},{2,1},{3,2},{4,3},{5,4},{6,5},{7,6},{0,7},{9,8},{10,9},{11,1... | collective-permute-start | bytes 19208 | tf_op jit(solution)/shard_map/ppermute | solution.py:15
  8.7 8.4 %copy-start.9 = (f32[2,128]{1,0:T(2,128)}, f32[2,128]{1,0:T(2,128)S(1)}, u32[]{:S(2)}) copy-start(f32[2,128]{1,0:T(2,128)S(1)} %subtract_subtract_fusion) | copy-start | bytes 3076
  9.0 8.1 %copy-start.2 = (bf16[8,100,2,128]{3,2,1,0:T(2,128)(2,1)S(1)}, bf16[8,100,2,128]{3,2,1,0:T(2,128)(2,1)}, u32[]{:S(2)}) copy-start(bf16[8,100,2,128]{3,2,1,0:T(2,128)(2,1)} %param.20) | copy-start | bytes 1228804
  18.5 2.4 %copy-start.4 = (bf16[3,8,100,100]{3,1,2,0:T(8,128)(2,1)S(1)}, bf16[3,8,100,100]{3,1,2,0:T(8,128)(2,1)}, u32[]{:S(2)}) copy-start(bf16[3,8,100,100]{3,1,2,0:T(8,128)(2,1)} %param.22) | copy-start | bytes 1440004
  19.4 1.5 %copy-start.3 = (bf16[2,8,100,2,128]{4,3,2,1,0:T(2,128)(2,1)S(1)}, bf16[2,8,100,2,128]{4,3,2,1,0:T(2,128)(2,1)}, u32[]{:S(2)}) copy-start(bf16[2,8,100,2,128]{4,3,2,1,0:T(2,128)(2,1)} %param.21) | copy-start | bytes 2457604
  19.4 13.6 %collective-permute-start.2 = (f32[8,100,1,128]{3,0,2,1:T(8,128)}, f32[8,100,1,128]{3,0,2,1:T(8,128)}, u32[]{:S(2)}, u32[]{:S(2)}) collective-permute-start(f32[8,100,1,128]{3,0,2,1:T(8,128)} %get-tuple-element.164), channel_id=1, source_target_pairs={{8,0},{16,8},{24,16},{9,1},{17,9},{25,17},{10,2},{18,10},{26,18},{... | collective-permute-start | bytes 1228808 | tf_op jit(solution)/shard_map/ppermute | solution.py:21
  22.3 2.8 %copy-start.6 = (s32[8,2,128]{2,1,0:T(2,128)S(1)}, s32[8,2,128]{2,1,0:T(2,128)}, u32[]{:S(2)}) copy-start(s32[8,2,128]{2,1,0:T(2,128)} %param.27) | copy-start | bytes 24580
  22.6 6.2 %collective-permute-start.3 = (f32[8,100,2,1]{1,0,3,2:T(8,128)S(1)}, f32[8,100,2,1]{1,0,3,2:T(8,128)}, u32[]{:S(2)}, u32[]{:S(2)}) collective-permute-start(f32[8,100,2,1]{1,0,3,2:T(8,128)S(1)} %copy.36), channel_id=1, source_target_pairs={{1,0},{2,1},{3,2},{4,3},{5,4},{6,5},{7,6},{0,7},{9,8},{10,9},{11,1... | collective-permute-start | bytes 19208 | tf_op jit(solution)/shard_map/ppermute | solution.py:15
  30.0 3.0 %copy-start.10 = (f32[2,128]{1,0:T(2,128)S(1)}, f32[2,128]{1,0:T(2,128)}, u32[]{:S(2)}) copy-start(f32[2,128]{1,0:T(2,128)} %copy-done.9) | copy-start | bytes 3076
  39.5 12.6 %copy-start.1 = (f32[8,100,1,128]{3,0,2,1:T(8,128)}, f32[8,100,1,128]{3,0,2,1:T(8,128)S(1)}, u32[]{:S(2)}) copy-start(f32[8,100,1,128]{3,0,2,1:T(8,128)S(1)} %get-tuple-element.161) | copy-start | bytes 1228804
  39.5 12.6 %collective-permute-start.4 = (f32[8,100,1,128]{3,0,2,1:T(8,128)}, f32[8,100,1,128]{3,0,2,1:T(8,128)}, u32[]{:S(2)}, u32[]{:S(2)}) collective-permute-start(f32[8,100,1,128]{3,0,2,1:T(8,128)} %get-tuple-element.162), channel_id=1, source_target_pairs={{8,0},{16,8},{24,16},{9,1},{17,9},{25,17},{10,2},{18,10},{26,18},{... | collective-permute-start | bytes 1228808 | tf_op jit(solution)/shard_map/ppermute | solution.py:21
  41.8 2.1 %collective-permute-start.5 = (f32[8,100,2,1]{1,0,3,2:T(8,128)}, f32[8,100,2,1]{1,0,3,2:T(8,128)}, u32[]{:S(2)}, u32[]{:S(2)}) collective-permute-start(f32[8,100,2,1]{1,0,3,2:T(8,128)} %copy.49), channel_id=1, source_target_pairs={{1,0},{2,1},{3,2},{4,3},{5,4},{6,5},{7,6},{0,7},{9,8},{10,9},{11,1... | collective-permute-start | bytes 19208 | tf_op jit(solution)/shard_map/ppermute | solution.py:15
  45.9 6.2 %copy-start.11 = (f32[2,128]{1,0:T(2,128)S(1)}, f32[2,128]{1,0:T(2,128)}, u32[]{:S(2)}) copy-start(f32[2,128]{1,0:T(2,128)} %copy-done.9) | copy-start | bytes 3076
  54.8 11.7 %collective-permute-start.6 = (f32[8,100,1,128]{3,0,2,1:T(8,128)}, f32[8,100,1,128]{3,0,2,1:T(8,128)}, u32[]{:S(2)}, u32[]{:S(2)}) collective-permute-start(f32[8,100,1,128]{3,0,2,1:T(8,128)} %get-tuple-element.160), channel_id=1, source_target_pairs={{8,0},{16,8},{24,16},{9,1},{17,9},{25,17},{10,2},{18,10},{26,18},{... | collective-permute-start | bytes 1228808 | tf_op jit(solution)/shard_map/ppermute | solution.py:21
  57.0 3.0 %collective-permute-start.7 = (f32[8,100,2,1]{1,0,3,2:T(8,128)}, f32[8,100,2,1]{1,0,3,2:T(8,128)}, u32[]{:S(2)}, u32[]{:S(2)}) collective-permute-start(f32[8,100,2,1]{1,0,3,2:T(8,128)} %copy.51), channel_id=1, source_target_pairs={{1,0},{2,1},{3,2},{4,3},{5,4},{6,5},{7,6},{0,7},{9,8},{10,9},{11,1... | collective-permute-start | bytes 19208 | tf_op jit(solution)/shard_map/ppermute | solution.py:15
  60.1 6.4 %copy-start = (f32[8,100,2,1]{3,0,2,1:T(8,128)S(1)}, f32[8,100,2,1]{3,0,2,1:T(8,128)}, u32[]{:S(2)}) copy-start(f32[8,100,2,1]{3,0,2,1:T(8,128)} %copy.50) | copy-start | bytes 19204
  66.5 0.7 copy-start.12
  74.1 0.9 copy-start.5
  75.2 0.7 copy-start.13
where the time goes:
time: 119 us; the launch traced here: 118 us
  blocking collectives  40.3 us (34%)
  waiting for transfers between devices  22.6 us (19%)
  local copies, waits for them, and re-layouts  21.5 us (18%)
  starting transfers between devices  13.5 us (11%)
  other arithmetic  8.79 us (7%)
  matrix products  7.96 us (7%)
  between operations  2.85 us (2%)
    psum x1, blocking collectives, per_device(): total = lax.psum(partial_value, ('lat', 'lon'))  40.3 us
    ppermute x4, waiting for transfers between devices, from_behind(): return lax.ppermute(block, axis, route)  20.2 us
    ppermute x4, starting transfers between devices, shifted(): return lax.ppermute(block, axis, route)  8.28 us
    dot_general x18, matrix products, transposed(): lax.dot_general(mats, right_side, (((1,), (1,)), ((0,), (0,))), preferred...  7.79 us
    ppermute x4, local copies, waits for them, and re-layouts, shifted(): return lax.ppermute(block, axis, route)  5.64 us
    add x3, other arithmetic, advect(): return (1.0 - clon - clat) * lam + clat * down + clon * right  5.49 us
    ppermute x4, starting transfers between devices, from_behind(): return lax.ppermute(block, axis, route)  5.25 us
    unnamed x36, local copies, waits for them, and re-layouts  5.18 us
  transfers between devices with their start and end apart: 8, of which 6 were waited for; matrix products, arithmetic and copies ran while one was open for 12% of the time, Pallas kernels for 0%

commit v1 on v0

--- a/solution.py
+++ b/solution.py
@@ -81,7 +81,7 @@
         precision=lax.Precision.HIGHEST,
         preferred_element_type=jnp.float32,
     )
-    total = lax.psum(partial_value, ("lat", "lon"))
+    total = lax.psum(lax.psum(partial_value, "lon"), "lat")
     share = REG_DEV
     grad = lax.dynamic_slice_in_dim(total, lax.axis_index(("lat", "lon")) * share, share, 0)
     return (lam.astype(jnp.bfloat16), grad)

time: 119 us -> 122 us (1.025)
  blocking collectives: 40.3 us -> 43.2 us
    psum x1 -> x2, blocking collectives: 40.3 us -> 43.2 us  [per_device(): total = lax.psum(lax.psum(partial_value, 'lon'), 'lat')]
where the time goes in v1:
time: 122 us; the launch traced here: 121 us
  blocking collectives  43.2 us (35%)
  waiting for transfers between devices  22.4 us (18%)
  local copies, waits for them, and re-layouts  21.6 us (18%)
  starting transfers between devices  13.5 us (11%)
  other arithmetic  8.82 us (7%)
  matrix products  7.96 us (7%)
  between operations  2.95 us (2%)
    psum x2, blocking collectives, per_device(): total = lax.psum(lax.psum(partial_value, 'lon'), 'lat')  43.2 us
    ppermute x4, waiting for transfers between devices, from_behind(): return lax.ppermute(block, axis, route)  20.1 us
    ppermute x4, starting transfers between devices, shifted(): return lax.ppermute(block, axis, route)  8.27 us
    dot_general x18, matrix products, transposed(): lax.dot_general(mats, right_side, (((1,), (1,)), ((0,), (0,))), preferred...  7.79 us
    ppermute x4, local copies, waits for them, and re-layouts, shifted(): return lax.ppermute(block, axis, route)  5.66 us
    add x3, other arithmetic, advect(): return (1.0 - clon - clat) * lam + clat * down + clon * right  5.49 us
    ppermute x4, starting transfers between devices, from_behind(): return lax.ppermute(block, axis, route)  5.25 us
    unnamed x36, local copies, waits for them, and re-layouts  5.21 us
  transfers between devices with their start and end apart: 8, of which 6 were waited for; matrix products, arithmetic and copies ran while one was open for 12% of the time, Pallas kernels for 0%

profile of v1, /device:TPU:0, one launch (start us, length us, event | category | flops | bytes accessed | tf_op | source)
XLA Modules:
  0.0 120.8 jit_solution(7805891861508252120)
XLA Ops:
  2.5 1.3 %collective-permute-start = (f32[8,100,1,128]{3,0,2,1:T(8,128)}, f32[8,100,1,128]{3,0,2,1:T(8,128)}, u32[]{:S(2)}, u32[]{:S(2)}) collective-permute-start(f32[8,100,1,128]{3,0,2,1:T(8,128)} %get-tuple-element.166), channel_id=1, source_target_pairs={{8,0},{16,8},{24,16},{9,1},{17,9},{25,17},{10,2},{18,10},{26,18},{... | collective-permute-start | bytes 1228808 | tf_op jit(solution)/shard_map/ppermute | solution.py:21
  4.2 4.5 %collective-permute-start.1 = (f32[8,100,2,1]{1,0,3,2:T(8,128)S(1)}, f32[8,100,2,1]{1,0,3,2:T(8,128)S(1)}, u32[]{:S(2)}, u32[]{:S(2)}) collective-permute-start(f32[8,100,2,1]{1,0,3,2:T(8,128)S(1)} %copy.34), channel_id=1, source_target_pairs={{1,0},{2,1},{3,2},{4,3},{5,4},{6,5},{7,6},{0,7},{9,8},{10,9},{11,1... | collective-permute-start | bytes 19208 | tf_op jit(solution)/shard_map/ppermute | solution.py:15
  10.5 6.6 %collective-permute-done = f32[8,100,1,128]{3,0,2,1:T(8,128)} collective-permute-done((f32[8,100,1,128]{3,0,2,1:T(8,128)}, f32[8,100,1,128]{3,0,2,1:T(8,128)}, u32[]{:S(2)}, u32[]{:S(2)}) %collective-permute-start) | collective-permute-done | bytes 409632 | tf_op jit(solution)/shard_map/ppermute | solution.py:21
  17.1 1.3 %fusion.65 = f32[8,100,2,128]{3,0,2,1:T(8,128)S(1)} fusion(f32[8,100,1,128]{3,0,2,1:T(8,128)} %collective-permute-done, f32[8,100,1,128]{3,0,2,1:T(8,128)S(1)} %get-tuple-element.165, f32[8,100,2,1]{3,0,2,1:T(8,128)S(1)} %copy.35, f32[8,100,2,127]{3,0,2,1:T(8,128)S(1)} %slice.99, f32[2,128]{1,0:T(2,128)S(1)} %copy-done.7, f32[2,128]{1,0:T(2,128)S(1)} %copy-done.8, ...), kind=kLoop, calls=%fused_computation.86 | loop fusion | flops 1638400 | bytes 2870272 | tf_op jit(solution)/shard_map/add | solution.py:27
  19.4 1.4 %collective-permute-start.2 = (f32[8,100,1,128]{3,0,2,1:T(8,128)}, f32[8,100,1,128]{3,0,2,1:T(8,128)}, u32[]{:S(2)}, u32[]{:S(2)}) collective-permute-start(f32[8,100,1,128]{3,0,2,1:T(8,128)} %get-tuple-element.164), channel_id=1, source_target_pairs={{8,0},{16,8},{24,16},{9,1},{17,9},{25,17},{10,2},{18,10},{26,18},{... | collective-permute-start | bytes 1228808 | tf_op jit(solution)/shard_map/ppermute | solution.py:21
  20.9 1.3 %fusion.79 = (bf16[1,8,100,2,128]{4,3,2,1,0:T(2,128)(2,1)}, bf16[1,8,100,2,128]{4,3,2,1,0:T(2,128)(2,1)S(1)}) fusion(bf16[2,8,100,2,128]{4,3,2,1,0:T(2,128)(2,1)S(1)} %copy-done.3), kind=kLoop, calls=%fused_computation.122 | loop fusion | bytes 1638400 | tf_op jit(solution)/shard_map/slice | solution.py:70
  22.6 2.4 %collective-permute-start.3 = (f32[8,100,2,1]{1,0,3,2:T(8,128)S(1)}, f32[8,100,2,1]{1,0,3,2:T(8,128)}, u32[]{:S(2)}, u32[]{:S(2)}) collective-permute-start(f32[8,100,2,1]{1,0,3,2:T(8,128)S(1)} %copy.36), channel_id=1, source_target_pairs={{1,0},{2,1},{3,2},{4,3},{5,4},{6,5},{7,6},{0,7},{9,8},{10,9},{11,1... | collective-permute-start | bytes 19208 | tf_op jit(solution)/shard_map/ppermute | solution.py:15
  30.1 2.9 %collective-permute-done.2 = f32[8,100,1,128]{3,0,2,1:T(8,128)} collective-permute-done((f32[8,100,1,128]{3,0,2,1:T(8,128)}, f32[8,100,1,128]{3,0,2,1:T(8,128)}, u32[]{:S(2)}, u32[]{:S(2)}) %collective-permute-start.2) | collective-permute-done | bytes 409632 | tf_op jit(solution)/shard_map/ppermute | solution.py:21
  33.0 1.4 %fusion.68 = f32[8,100,256]{2,0,1:T(8,128)S(1)} fusion(f32[8,100,1,128]{3,0,2,1:T(8,128)} %collective-permute-done.2, f32[8,100,1,128]{3,0,2,1:T(8,128)} %get-tuple-element.163, f32[8,100,2,1]{3,0,2,1:T(8,128)S(1)} %copy.37, f32[8,100,2,127]{3,0,2,1:T(8,128)S(1)} %slice.103, f32[8,100,2,128]{3,0,2,1:T(8,128)S(1)} %fusion.65, f32[2,128]{1,0:T(2,128)S(1)} %copy-done.7, ...), kind=kLoop, calls=%fused_computation.91 | loop fusion | flops 1433600 | bytes 3279872 | tf_op jit(solution)/shard_map/reshape | solution.py:46
  34.4 1.3 %conditional.6 = (f32[8,100,256]{2,1,0:T(8,128)S(1)}) conditional(s32[]{:T(128)} %convert_element_type.102, (f32[8,100,256]{2,0,1:T(8,128)S(1)}) %tuple.65, (s32[8,1,256]{2,0,1:T(8,128)S(1)}, f32[8,100,256]{2,0,1:T(8,128)S(1)}, bf16[8,100,100]{1,2,0:T(8,128)(2,1)S(1)}, bf16[8,100,256]{2,0,1:T(8,128)(2,1)S(1)}) %tuple.94), branch_computations={%region_3.4_spmd, %region_4.5_spmd} | conditional | flops 125749248 | bytes 7865096 | solution.py:59
  35.8 1.3 %conditional.7 = (f32[8,100,256]{2,1,0:T(8,128)S(1)}) conditional(s32[]{:T(128)} %convert_element_type.101, f32[8,100,256]{2,1,0:T(8,128)S(1)} %get-tuple-element.170, (s32[8,1,256]{2,0,1:T(8,128)S(1)}, f32[8,100,256]{2,1,0:T(8,128)S(1)}, bf16[8,100,100]{1,2,0:T(8,128)(2,1)S(1)}, bf16[8,100,256]{2,0,1:T(8,128)(2,1)S(1)}) %tuple.98), branch_computations={%region_5.6_spmd, %region_6.7_spmd} | conditional | flops 125954048 | bytes 7865096 | solution.py:59
  37.1 1.3 %conditional.8 = (f32[8,100,256]{2,1,0:T(8,128)S(1)}) conditional(s32[]{:T(128)} %convert_element_type.100, f32[8,100,256]{2,1,0:T(8,128)S(1)} %get-tuple-element.171, (s32[8,1,256]{2,0,1:T(8,128)S(1)}, f32[8,100,256]{2,1,0:T(8,128)S(1)}, bf16[8,100,100]{1,2,0:T(8,128)(2,1)S(1)}, bf16[8,100,256]{2,0,1:T(8,128)(2,1)S(1)}) %tuple.96), branch_computations={%region_7.8_spmd, %region_8.9_spmd} | conditional | flops 125954048 | bytes 7865096 | solution.py:59
  42.6 1.3 %collective-permute-done.5 = f32[8,100,2,1]{1,0,3,2:T(8,128)} collective-permute-done((f32[8,100,2,1]{1,0,3,2:T(8,128)}, f32[8,100,2,1]{1,0,3,2:T(8,128)}, u32[]{:S(2)}, u32[]{:S(2)}) %collective-permute-start.5) | collective-permute-done | bytes 6432 | tf_op jit(solution)/shard_map/ppermute | solution.py:15
  43.9 2.0 %copy.50 = f32[8,100,2,1]{3,0,2,1:T(8,128)} copy(f32[8,100,2,1]{1,0,3,2:T(8,128)} %collective-permute-done.5) | data formatting | bytes 12800 | tf_op jit(solution)/shard_map/ppermute | solution.py:15
  45.9 6.2 %collective-permute-done.4 = f32[8,100,1,128]{3,0,2,1:T(8,128)} collective-permute-done((f32[8,100,1,128]{3,0,2,1:T(8,128)}, f32[8,100,1,128]{3,0,2,1:T(8,128)}, u32[]{:S(2)}, u32[]{:S(2)}) %collective-permute-start.4) | collective-permute-done | bytes 409632 | tf_op jit(solution)/shard_map/ppermute | solution.py:21
  52.2 1.7 %multiply_add_fusion = f32[8,100,2,128]{3,0,2,1:T(8,128)S(1)} fusion(f32[8,100,1,128]{3,0,2,1:T(8,128)} %collective-permute-done.4, f32[8,100,1,128]{3,0,2,1:T(8,128)S(1)} %get-tuple-element.161, f32[2,128]{1,0:T(2,128)S(1)} %copy-done.7, f32[2,128]{1,0:T(2,128)S(1)} %copy-done.8, f32[2,128]{1,0:T(2,128)S(1)} %copy-done.11, f32[8,100,2,1]{3,0,2,1:T(8,128)} %copy.50, ...), kind=kLoop, calls=%fused_computation.107 | loop fusion | flops 1433600 | bytes 3279872 | tf_op jit(solution)/shard_map/add | solution.py:27
  60.1 2.1 %copy.52 = f32[8,100,2,1]{3,0,2,1:T(8,128)} copy(f32[8,100,2,1]{1,0,3,2:T(8,128)} %collective-permute-done.7) | data formatting | bytes 12800 | tf_op jit(solution)/shard_map/ppermute | solution.py:15
  62.2 4.3 %collective-permute-done.6 = f32[8,100,1,128]{3,0,2,1:T(8,128)} collective-permute-done((f32[8,100,1,128]{3,0,2,1:T(8,128)}, f32[8,100,1,128]{3,0,2,1:T(8,128)}, u32[]{:S(2)}, u32[]{:S(2)}) %collective-permute-start.6) | collective-permute-done | bytes 409632 | tf_op jit(solution)/shard_map/ppermute | solution.py:21
  67.2 2.5 %fusion.71 = f32[8,100,256]{2,0,1:T(8,128)S(1)} fusion(f32[8,100,1,128]{3,0,2,1:T(8,128)} %collective-permute-done.6, f32[8,100,1,128]{3,0,2,1:T(8,128)} %get-tuple-element.159, f32[8,100,2,1]{3,0,2,1:T(8,128)} %copy.52, f32[8,100,2,127]{3,0,2,1:T(8,128)} %slice.111, f32[8,100,256]{2,1,0:T(8,128)S(1)} %get-tuple-element.172, ...), kind=kLoop, calls=%fused_computation.98 | loop fusion | flops 2867200 | bytes 4918272 | tf_op jit(solution)/shard_map/add | solution.py:27
  69.7 1.5 %conditional.9 = (f32[8,100,256]{2,1,0:T(8,128)S(1)}) conditional(s32[]{:T(128)} %convert_element_type.102, (f32[8,100,256]{2,0,1:T(8,128)S(1)}) %tuple.66, (s32[8,1,256]{2,0,1:T(8,128)S(1)}, f32[8,100,256]{2,0,1:T(8,128)S(1)}, bf16[8,100,100]{1,2,0:T(8,128)(2,1)S(1)}, bf16[8,100,256]{2,0,1:T(8,128)(2,1)S(1)}) %tuple.95), branch_computations={%region_9.10_spmd, %region_10.11_spmd} | conditional | flops 125749248 | bytes 7865096 | solution.py:59
  71.2 1.3 %conditional.10 = (f32[8,100,256]{2,1,0:T(8,128)S(1)}) conditional(s32[]{:T(128)} %convert_element_type.101, f32[8,100,256]{2,1,0:T(8,128)S(1)} %get-tuple-element.173, (s32[8,1,256]{2,0,1:T(8,128)S(1)}, f32[8,100,256]{2,1,0:T(8,128)S(1)}, bf16[8,100,100]{1,2,0:T(8,128)(2,1)S(1)}, bf16[8,100,256]{2,0,1:T(8,128)(2,1)S(1)}) %tuple.99), branch_computations={%region_11.12_spmd, %region_12.13_spmd} | conditional | flops 125954048 | bytes 7865096 | solution.py:59
  72.6 1.3 %conditional.11 = (f32[8,100,256]{2,1,0:T(8,128)S(1)}) conditional(s32[]{:T(128)} %convert_element_type.100, f32[8,100,256]{2,1,0:T(8,128)S(1)} %get-tuple-element.174, (s32[8,1,256]{2,0,1:T(8,128)S(1)}, f32[8,100,256]{2,1,0:T(8,128)S(1)}, bf16[8,100,100]{1,2,0:T(8,128)(2,1)S(1)}, bf16[8,100,256]{2,0,1:T(8,128)(2,1)S(1)}) %tuple.97), branch_computations={%region_13.14_spmd, %region_14.15_spmd} | conditional | flops 125954048 | bytes 7865096 | solution.py:59
  76.1 26.0 %psum.14 = f32[32,100]{1,0:T(8,128)S(1)} all-reduce(f32[32,100]{1,0:T(8,128)S(1)} %fusion.77), channel_id=1, replica_groups=mesh['lat'=4,'lon'=8] {'lon'}, use_global_device_ids=true, to_apply=%region_15.16 | all-reduce | flops 3200 | bytes 25600 | tf_op jit(solution)/shard_map/psum | solution.py:84
  102.1 17.2 %psum.15 = f32[32,100]{1,0:T(8,128)S(1)} all-reduce(f32[32,100]{1,0:T(8,128)S(1)} %psum.14), channel_id=1, replica_groups=mesh['lat'=4,'lon'=8] {'lat'}, use_global_device_ids=true, to_apply=%region_16.17 | all-reduce | flops 3200 | bytes 25600 | tf_op jit(solution)/shard_map/psum | solution.py:84
  (93 shorter events, 31.0 us)
Async XLA Ops:
  2.5 14.6 %collective-permute-start = (f32[8,100,1,128]{3,0,2,1:T(8,128)}, f32[8,100,1,128]{3,0,2,1:T(8,128)}, u32[]{:S(2)}, u32[]{:S(2)}) collective-permute-start(f32[8,100,1,128]{3,0,2,1:T(8,128)} %get-tuple-element.166), channel_id=1, source_target_pairs={{8,0},{16,8},{24,16},{9,1},{17,9},{25,17},{10,2},{18,10},{26,18},{... | collective-permute-start | bytes 1228808 | tf_op jit(solution)/shard_map/ppermute | solution.py:21
  3.8 4.9 %copy-start.7 = (f32[2,128]{1,0:T(2,128)S(1)}, f32[2,128]{1,0:T(2,128)}, u32[]{:S(2)}) copy-start(f32[2,128]{1,0:T(2,128)} %param.23) | copy-start | bytes 3076
  3.8 4.9 %copy-start.8 = (f32[2,128]{1,0:T(2,128)S(1)}, f32[2,128]{1,0:T(2,128)}, u32[]{:S(2)}) copy-start(f32[2,128]{1,0:T(2,128)} %param.24) | copy-start | bytes 3076
  4.2 5.9 %collective-permute-start.1 = (f32[8,100,2,1]{1,0,3,2:T(8,128)S(1)}, f32[8,100,2,1]{1,0,3,2:T(8,128)S(1)}, u32[]{:S(2)}, u32[]{:S(2)}) collective-permute-start(f32[8,100,2,1]{1,0,3,2:T(8,128)S(1)} %copy.34), channel_id=1, source_target_pairs={{1,0},{2,1},{3,2},{4,3},{5,4},{6,5},{7,6},{0,7},{9,8},{10,9},{11,1... | collective-permute-start | bytes 19208 | tf_op jit(solution)/shard_map/ppermute | solution.py:15
  8.7 8.4 %copy-start.9 = (f32[2,128]{1,0:T(2,128)}, f32[2,128]{1,0:T(2,128)S(1)}, u32[]{:S(2)}) copy-start(f32[2,128]{1,0:T(2,128)S(1)} %subtract_subtract_fusion) | copy-start | bytes 3076
  9.0 8.1 %copy-start.2 = (bf16[8,100,2,128]{3,2,1,0:T(2,128)(2,1)S(1)}, bf16[8,100,2,128]{3,2,1,0:T(2,128)(2,1)}, u32[]{:S(2)}) copy-start(bf16[8,100,2,128]{3,2,1,0:T(2,128)(2,1)} %param.20) | copy-start | bytes 1228804
  18.5 2.4 %copy-start.4 = (bf16[3,8,100,100]{3,1,2,0:T(8,128)(2,1)S(1)}, bf16[3,8,100,100]{3,1,2,0:T(8,128)(2,1)}, u32[]{:S(2)}) copy-start(bf16[3,8,100,100]{3,1,2,0:T(8,128)(2,1)} %param.22) | copy-start | bytes 1440004
  19.4 1.5 %copy-start.3 = (bf16[2,8,100,2,128]{4,3,2,1,0:T(2,128)(2,1)S(1)}, bf16[2,8,100,2,128]{4,3,2,1,0:T(2,128)(2,1)}, u32[]{:S(2)}) copy-start(bf16[2,8,100,2,128]{4,3,2,1,0:T(2,128)(2,1)} %param.21) | copy-start | bytes 2457604
  19.4 13.6 %collective-permute-start.2 = (f32[8,100,1,128]{3,0,2,1:T(8,128)}, f32[8,100,1,128]{3,0,2,1:T(8,128)}, u32[]{:S(2)}, u32[]{:S(2)}) collective-permute-start(f32[8,100,1,128]{3,0,2,1:T(8,128)} %get-tuple-element.164), channel_id=1, source_target_pairs={{8,0},{16,8},{24,16},{9,1},{17,9},{25,17},{10,2},{18,10},{26,18},{... | collective-permute-start | bytes 1228808 | tf_op jit(solution)/shard_map/ppermute | solution.py:21
  22.2 2.8 %copy-start.6 = (s32[8,2,128]{2,1,0:T(2,128)S(1)}, s32[8,2,128]{2,1,0:T(2,128)}, u32[]{:S(2)}) copy-start(s32[8,2,128]{2,1,0:T(2,128)} %param.27) | copy-start | bytes 24580
  22.6 6.3 %collective-permute-start.3 = (f32[8,100,2,1]{1,0,3,2:T(8,128)S(1)}, f32[8,100,2,1]{1,0,3,2:T(8,128)}, u32[]{:S(2)}, u32[]{:S(2)}) collective-permute-start(f32[8,100,2,1]{1,0,3,2:T(8,128)S(1)} %copy.36), channel_id=1, source_target_pairs={{1,0},{2,1},{3,2},{4,3},{5,4},{6,5},{7,6},{0,7},{9,8},{10,9},{11,1... | collective-permute-start | bytes 19208 | tf_op jit(solution)/shard_map/ppermute | solution.py:15
  30.1 2.9 %copy-start.10 = (f32[2,128]{1,0:T(2,128)S(1)}, f32[2,128]{1,0:T(2,128)}, u32[]{:S(2)}) copy-start(f32[2,128]{1,0:T(2,128)} %copy-done.9) | copy-start | bytes 3076
  39.6 12.6 %copy-start.1 = (f32[8,100,1,128]{3,0,2,1:T(8,128)}, f32[8,100,1,128]{3,0,2,1:T(8,128)S(1)}, u32[]{:S(2)}) copy-start(f32[8,100,1,128]{3,0,2,1:T(8,128)S(1)} %get-tuple-element.161) | copy-start | bytes 1228804
  39.6 12.6 %collective-permute-start.4 = (f32[8,100,1,128]{3,0,2,1:T(8,128)}, f32[8,100,1,128]{3,0,2,1:T(8,128)}, u32[]{:S(2)}, u32[]{:S(2)}) collective-permute-start(f32[8,100,1,128]{3,0,2,1:T(8,128)} %get-tuple-element.162), channel_id=1, source_target_pairs={{8,0},{16,8},{24,16},{9,1},{17,9},{25,17},{10,2},{18,10},{26,18},{... | collective-permute-start | bytes 1228808 | tf_op jit(solution)/shard_map/ppermute | solution.py:21
  41.8 2.1 %collective-permute-start.5 = (f32[8,100,2,1]{1,0,3,2:T(8,128)}, f32[8,100,2,1]{1,0,3,2:T(8,128)}, u32[]{:S(2)}, u32[]{:S(2)}) collective-permute-start(f32[8,100,2,1]{1,0,3,2:T(8,128)} %copy.49), channel_id=1, source_target_pairs={{1,0},{2,1},{3,2},{4,3},{5,4},{6,5},{7,6},{0,7},{9,8},{10,9},{11,1... | collective-permute-start | bytes 19208 | tf_op jit(solution)/shard_map/ppermute | solution.py:15
  45.9 6.2 %copy-start.11 = (f32[2,128]{1,0:T(2,128)S(1)}, f32[2,128]{1,0:T(2,128)}, u32[]{:S(2)}) copy-start(f32[2,128]{1,0:T(2,128)} %copy-done.9) | copy-start | bytes 3076
  54.8 11.7 %collective-permute-start.6 = (f32[8,100,1,128]{3,0,2,1:T(8,128)}, f32[8,100,1,128]{3,0,2,1:T(8,128)}, u32[]{:S(2)}, u32[]{:S(2)}) collective-permute-start(f32[8,100,1,128]{3,0,2,1:T(8,128)} %get-tuple-element.160), channel_id=1, source_target_pairs={{8,0},{16,8},{24,16},{9,1},{17,9},{25,17},{10,2},{18,10},{26,18},{... | collective-permute-start | bytes 1228808 | tf_op jit(solution)/shard_map/ppermute | solution.py:21
  57.0 3.1 %collective-permute-start.7 = (f32[8,100,2,1]{1,0,3,2:T(8,128)}, f32[8,100,2,1]{1,0,3,2:T(8,128)}, u32[]{:S(2)}, u32[]{:S(2)}) collective-permute-start(f32[8,100,2,1]{1,0,3,2:T(8,128)} %copy.51), channel_id=1, source_target_pairs={{1,0},{2,1},{3,2},{4,3},{5,4},{6,5},{7,6},{0,7},{9,8},{10,9},{11,1... | collective-permute-start | bytes 19208 | tf_op jit(solution)/shard_map/ppermute | solution.py:15
  60.1 6.4 %copy-start = (f32[8,100,2,1]{3,0,2,1:T(8,128)S(1)}, f32[8,100,2,1]{3,0,2,1:T(8,128)}, u32[]{:S(2)}) copy-start(f32[8,100,2,1]{3,0,2,1:T(8,128)} %copy.50) | copy-start | bytes 19204
  66.5 0.7 copy-start.12
  74.2 0.9 copy-start.5
  75.2 0.7 copy-start.13
